TPU v7x, 32 devices: a whole 2x2x4 slice. The times are simulated.
32 devices in a mesh: pipe: 4 (over x, core), mp: 8 (over z, y).
Axes of the slice: x: 2, y: 2, z: 4, core: 2. Of those that a mesh axis runs over, the one named last changes fastest.
Arguments:
- hidden_in: bfloat16 [32, 8192], P(None, 'mp'), may hold values from -24000 to 24000
- lengths: int32 [32], replicated, may hold values from 1 to 256
- assign: int32 [32], replicated, may hold values from 0 to 31, each once
- token_ids: int32 [32], replicated, may hold values from 0 to 12287
- attn_gain: bfloat16 [4, 8192], P('pipe', 'mp'), may hold values from 0.099609375 to 1.8984375
- qkv_weight: bfloat16 [4, 8192, 5120], P('pipe', 'mp'), may hold values from -0.0625 to 0.0625
- qkv_bias: bfloat16 [4, 5120], P('pipe'), may hold values from -3 to 3
- out_weight: bfloat16 [4, 4096, 8192], P('pipe', None, 'mp'), may hold values from -0.375 to 0.375
- kv_cache: bfloat16 [4, 32, 2, 4, 256, 128], P('pipe', 'mp'), may hold values from -120 to 120
- final_gain: bfloat16 [8192], P('mp'), may hold values from 0.099609375 to 1.8984375
- head_weight: bfloat16 [8192, 12288], P(None, ('pipe', 'mp')), may hold values from -0.9923308 to 0.9923308
Outputs:
- logprobs: float32 [32, 12288], P(None, ('pipe', 'mp'))
- chosen: float32 [32], replicated
Inputs may be any that keep to these rules, and one draw needn't show every extreme that they name: `assign`: a permutation of the 32 requests.
All inputs are finite; a program needn't handle non-finite values.
Results may differ from a plain program's by a relative error of at most 0.0017.
Values may be sent and summed in bfloat16 or wider, within the bound.
No kernel may reach another device: no remote copies, remote signals or barrier semaphores. Data moves between devices by JAX's collectives and lax.ppermute only.
A program may use at most 64 MiB of HBM per device.

v0:
```python
import jax
import jax.numpy as jnp
from jax import lax
from jax.sharding import PartitionSpec as P

D = 8192
HEADS = 32
KV_HEADS = 4
HEAD_DIM = 128
MICRO = 4
MB_ROWS = 8
EPS = 1e-06
THETA = 1000000.0


def from_behind(block, axis, distance):
    devices = range(lax.axis_size(axis))
    route = [(i - distance, i) for i in devices if i - distance in devices]
    return lax.ppermute(block, axis, route)


def from_root(value, axis, root):
    mine = lax.axis_index(axis) == root
    return lax.psum(jnp.where(mine, value, jnp.zeros_like(value)), axis)


def rotate(values_in, positions):
    half_dim = values_in.shape[-1] // 2
    frequency = THETA ** (-jnp.arange(half_dim).astype(jnp.float32) * 2.0 / values_in.shape[-1])
    angles = positions.astype(jnp.float32)[:, None, None] * frequency[None, None, :]
    front_half = values_in[..., :half_dim]
    back_half = values_in[..., half_dim:]
    cosine = jnp.cos(angles)
    sine_part = jnp.sin(angles)
    return jnp.concatenate(
        [front_half * cosine - back_half * sine_part, back_half * cosine + front_half * sine_part],
        axis=-1,
    )


def local(
    hidden_in,
    lengths,
    assign,
    token_ids,
    attn_gain,
    qkv_weight,
    qkv_bias,
    out_weight,
    kv_cache,
    final_gain,
    head_weight,
):
    sections = lax.axis_size("pipe")
    section_index = lax.axis_index("pipe")
    local_count = kv_cache.shape[1]
    query_cols = HEADS * HEAD_DIM
    key_cols = KV_HEADS * HEAD_DIM
    group_size = HEADS // KV_HEADS
    scale_factor = HEAD_DIM ** (-0.5)
    own_ids = lax.axis_index("mp") * local_count + jnp.arange(local_count, dtype=jnp.int32)
    slot_ids = jnp.arange(assign.shape[0], dtype=jnp.int32)
    slot_of = jnp.zeros_like(assign).at[assign].set(slot_ids)
    every_row = slot_of % MB_ROWS
    every_batch = slot_of // MB_ROWS
    own_slots = slot_of[own_ids]
    own_lengths = lengths[own_ids]
    own_rows = own_slots % MB_ROWS
    own_batch = own_slots // MB_ROWS
    visible = jnp.arange(kv_cache.shape[4], dtype=jnp.int32)[None, :] < own_lengths[:, None]
    gain_row = attn_gain[0].astype(jnp.float32)
    weight_in = qkv_weight[0]
    bias_row = qkv_bias[0].astype(jnp.float32)
    weight_out = out_weight[0]
    cache_rows = kv_cache[0]
    slot_table = assign.reshape(MICRO, MB_ROWS)
    row_slots = jnp.arange(MB_ROWS, dtype=jnp.int32)

    def attend_one(request_item):
        queries_one, key_one, value_one, cache_one, visible_one, present_one = request_item

        def compute(unused):
            scores = (
                jnp.einsum(
                    "kgd,kjd->kgj", queries_one, cache_one[0], preferred_element_type=jnp.float32
                )
                * scale_factor
            )
            self_score = (
                jnp.einsum("kgd,kd->kg", queries_one, key_one, preferred_element_type=jnp.float32)
                * scale_factor
            )
            key_mask = visible_one[None, None, :]
            row_top = jnp.maximum(jnp.max(jnp.where(key_mask, scores, -1e30), axis=-1), self_score)
            weights = jnp.where(key_mask, jnp.exp(scores - row_top[..., None]), 0.0)
            self_weight = jnp.exp(self_score - row_top)
            row_total = jnp.sum(weights, axis=-1) + self_weight
            summed = jnp.einsum(
                "kgj,kjd->kgd",
                weights.astype(jnp.bfloat16),
                cache_one[1],
                preferred_element_type=jnp.float32,
            )
            summed = summed + jnp.einsum(
                "kg,kd->kgd",
                self_weight.astype(jnp.bfloat16),
                value_one,
                preferred_element_type=jnp.float32,
            )
            return (summed / row_total[..., None]).astype(jnp.bfloat16).reshape(query_cols)

        def nothing(unused):
            return jnp.zeros((query_cols,), jnp.bfloat16)

        return lax.cond(present_one, compute, nothing, 0)

    def apply_layer(rows_in, batch_index):
        current = rows_in.astype(jnp.float32)
        squares = jnp.sum(current * current, axis=1)
        scaled = (current * gain_row).astype(jnp.bfloat16)
        partial_cols = jnp.dot(scaled, weight_in, preferred_element_type=jnp.float32)
        squares_all = lax.psum(squares, "mp")
        share_cols = lax.psum_scatter(partial_cols, "mp", scatter_dimension=1, tiled=True)
        share_width = share_cols.shape[1]
        share_bias = lax.dynamic_slice_in_dim(
            bias_row, lax.axis_index("mp") * share_width, share_width, 0
        )
        share_cols = share_cols * lax.rsqrt(squares_all / D + EPS)[:, None] + share_bias
        wanted = (
            (every_row[:, None] == row_slots[None, :]) & (every_batch[:, None] == batch_index)
        ).astype(jnp.float32)
        routed_rows = jnp.dot(wanted, share_cols, precision=lax.Precision.HIGHEST)
        picked = lax.all_to_all(routed_rows, "mp", split_axis=0, concat_axis=1, tiled=True)
        queries = rotate(
            picked[:, :query_cols].reshape(local_count, HEADS, HEAD_DIM), own_lengths
        ).astype(jnp.bfloat16)
        queries = queries.reshape(local_count, KV_HEADS, group_size, HEAD_DIM)
        key_new = rotate(
            picked[:, query_cols : query_cols + key_cols].reshape(local_count, KV_HEADS, HEAD_DIM),
            own_lengths,
        ).astype(jnp.bfloat16)
        value_new = (
            picked[:, query_cols + key_cols :]
            .reshape(local_count, KV_HEADS, HEAD_DIM)
            .astype(jnp.bfloat16)
        )
        present = own_batch == batch_index
        attended = lax.map(attend_one, (queries, key_new, value_new, cache_rows, visible, present))
        placing = ((own_rows[:, None] == row_slots[None, :]) & present[:, None]).astype(
            jnp.bfloat16
        )
        spread = jnp.dot(placing.T, attended, preferred_element_type=jnp.float32)
        gathered = lax.psum(spread.astype(jnp.bfloat16), "mp")
        update = jnp.dot(gathered, weight_out, preferred_element_type=jnp.float32)
        return (current + update).astype(jnp.bfloat16)

    def advance(turn_index, state_pair):
        outgoing, finished = state_pair
        incoming = from_behind(outgoing, "pipe", 1)
        offset = turn_index - section_index
        batch_index = jnp.clip(offset, 0, MICRO - 1)
        members = lax.dynamic_index_in_dim(slot_table, batch_index, 0, keepdims=False)
        entering = jnp.take(hidden_in, members, axis=0)
        rows_in = jnp.where(section_index == 0, entering, incoming)
        inside = (offset >= 0) & (offset < MICRO)
        rows_out = apply_layer(rows_in, jnp.where(inside, batch_index, -1))
        storing = inside & (section_index == sections - 1)
        placed = lax.dynamic_update_slice_in_dim(finished, rows_out, batch_index * MB_ROWS, 0)
        return (rows_out, jnp.where(storing, placed, finished))

    outgoing = jnp.zeros((MB_ROWS, hidden_in.shape[1]), jnp.bfloat16)
    finished = jnp.zeros(hidden_in.shape, jnp.bfloat16)
    outgoing, finished = lax.fori_loop(0, MICRO + sections - 1, advance, (outgoing, finished))
    final_rows = from_root(finished, "pipe", sections - 1)
    current = final_rows.astype(jnp.float32)
    squares = lax.psum(jnp.sum(current * current, axis=1), "mp")
    normed = (
        current * final_gain.astype(jnp.float32) * lax.rsqrt(squares / D + EPS)[:, None]
    ).astype(jnp.bfloat16)
    logits = jnp.dot(
        lax.all_gather(normed, "mp", axis=1, tiled=True),
        head_weight,
        preferred_element_type=jnp.float32,
    )
    vocab_width = head_weight.shape[1]
    vocab_ids = lax.axis_index(("pipe", "mp")) * vocab_width + jnp.arange(
        vocab_width, dtype=jnp.int32
    )
    targets = token_ids[assign]
    matches = vocab_ids[None, :] == targets[:, None]
    picked_local = jnp.sum(jnp.where(matches, logits, 0.0), axis=1)
    local_top = jnp.max(logits, axis=1)
    row_top = lax.pmax(local_top, ("pipe", "mp"))
    local_total = jnp.sum(jnp.exp(logits - row_top[:, None]), axis=1)
    row_total, picked = lax.psum((local_total, picked_local), ("pipe", "mp"))
    log_total = row_top + jnp.log(row_total)
    return (logits - log_total[:, None], picked - log_total)


def solution(mesh):
    return jax.shard_map(
        local,
        mesh=mesh,
        in_specs=(
            P(None, "mp"),
            P(),
            P(),
            P(),
            P("pipe", "mp"),
            P("pipe", "mp", None),
            P("pipe", None),
            P("pipe", None, "mp"),
            P("pipe", "mp", None, None, None, None),
            P("mp"),
            P(None, ("pipe", "mp")),
        ),
        out_specs=(P(None, ("pipe", "mp")), P()),
        check_vma=False,
    )
```

profile of v0, /device:TPU:0, one launch (start us, length us, event | category | flops | bytes accessed | tf_op | source)
XLA Modules:
  0.0 1336.8 jit_solution(10831050884700243807)
XLA Ops:
  13.6 1144.0 %while.53 = (s32[]{:T(128)}, bf16[8,1024]{1,0:T(8,128)(2,1)S(1)}, bf16[32,1024]{1,0:T(8,128)(2,1)S(1)}, pred[]{:T(512)}, s32[]{:T(128)}, /*index=5*/s32[4,8]{1,0...) while((s32[]{:T(128)}, bf16[8,1024]{1,0:T(8,128)(2,1)S(1)}, ...), condition=%wide.region_12.13_spmd.clone.clone, body=%wide.region_1.12_spmd.clone.clone.sunk | while | flops 157849424 | bytes 22136348 | solution.py:173
  24.2 22.5 %psum.66 = f32[8]{0:T(128)S(1)} all-reduce(f32[8]{0:T(128)S(1)} %get-tuple-element.929), channel_id=1, replica_groups=mesh['pipe'=4,'mp'=8] {'mp'}, use_global_device_ids=true, to_apply=%region_4.4 | all-reduce | flops 8 | bytes 64 | tf_op jit(solution)/shard_map/while/body/eval_jaxpr/psum | solution.py:122
  46.7 36.4 %reduce-scatter.2.cloned.1.call-done = f32[8,640]{1,0:T(8,128)} async-done(((f32[8,5120]{1,0:T(8,128)}), f32[8,640]{1,0:T(8,128)}) %reduce-scatter.2.cloned.1.call-update) | async-done | bytes 20496 | tf_op jit(solution)/shard_map/while/body/eval_jaxpr/reduce_scatter | solution.py:123
  108.5 65.4 %all-reduce.6.cloned.1.call-done = bf16[8,4096]{1,0:T(8,128)(2,1)} async-done(((bf16[8,4096]{1,0:T(8,128)(2,1)}), bf16[8,4096]{1,0:T(8,128)(2,1)}) %all-reduce.6.cloned.1.call-update) | async-done | bytes 65552 | tf_op jit(solution)/shard_map/while/body/eval_jaxpr/psum | solution.py:153
  188.0 20.4 %psum.66 = f32[8]{0:T(128)S(1)} all-reduce(f32[8]{0:T(128)S(1)} %get-tuple-element.929), channel_id=1, replica_groups=mesh['pipe'=4,'mp'=8] {'mp'}, use_global_device_ids=true, to_apply=%region_4.4 | all-reduce | flops 8 | bytes 64 | tf_op jit(solution)/shard_map/while/body/eval_jaxpr/psum | solution.py:122
  208.4 36.8 %reduce-scatter.2.cloned.1.call-done = f32[8,640]{1,0:T(8,128)} async-done(((f32[8,5120]{1,0:T(8,128)}), f32[8,640]{1,0:T(8,128)}) %reduce-scatter.2.cloned.1.call-update) | async-done | bytes 20496 | tf_op jit(solution)/shard_map/while/body/eval_jaxpr/reduce_scatter | solution.py:123
  270.7 65.3 %all-reduce.6.cloned.1.call-done = bf16[8,4096]{1,0:T(8,128)(2,1)} async-done(((bf16[8,4096]{1,0:T(8,128)(2,1)}), bf16[8,4096]{1,0:T(8,128)(2,1)}) %all-reduce.6.cloned.1.call-update) | async-done | bytes 65552 | tf_op jit(solution)/shard_map/while/body/eval_jaxpr/psum | solution.py:153
  350.0 20.4 %psum.66 = f32[8]{0:T(128)S(1)} all-reduce(f32[8]{0:T(128)S(1)} %get-tuple-element.929), channel_id=1, replica_groups=mesh['pipe'=4,'mp'=8] {'mp'}, use_global_device_ids=true, to_apply=%region_4.4 | all-reduce | flops 8 | bytes 64 | tf_op jit(solution)/shard_map/while/body/eval_jaxpr/psum | solution.py:122
  370.4 36.8 %reduce-scatter.2.cloned.1.call-done = f32[8,640]{1,0:T(8,128)} async-done(((f32[8,5120]{1,0:T(8,128)}), f32[8,640]{1,0:T(8,128)}) %reduce-scatter.2.cloned.1.call-update) | async-done | bytes 20496 | tf_op jit(solution)/shard_map/while/body/eval_jaxpr/reduce_scatter | solution.py:123
  427.2 73.7 %all-reduce.6.cloned.1.call-done = bf16[8,4096]{1,0:T(8,128)(2,1)} async-done(((bf16[8,4096]{1,0:T(8,128)(2,1)}), bf16[8,4096]{1,0:T(8,128)(2,1)}) %all-reduce.6.cloned.1.call-update) | async-done | bytes 65552 | tf_op jit(solution)/shard_map/while/body/eval_jaxpr/psum | solution.py:153
  515.0 20.4 %psum.66 = f32[8]{0:T(128)S(1)} all-reduce(f32[8]{0:T(128)S(1)} %get-tuple-element.929), channel_id=1, replica_groups=mesh['pipe'=4,'mp'=8] {'mp'}, use_global_device_ids=true, to_apply=%region_4.4 | all-reduce | flops 8 | bytes 64 | tf_op jit(solution)/shard_map/while/body/eval_jaxpr/psum | solution.py:122
  535.3 36.8 %reduce-scatter.2.cloned.1.call-done = f32[8,640]{1,0:T(8,128)} async-done(((f32[8,5120]{1,0:T(8,128)}), f32[8,640]{1,0:T(8,128)}) %reduce-scatter.2.cloned.1.call-update) | async-done | bytes 20496 | tf_op jit(solution)/shard_map/while/body/eval_jaxpr/reduce_scatter | solution.py:123
  592.1 72.1 %all-reduce.6.cloned.1.call-done = bf16[8,4096]{1,0:T(8,128)(2,1)} async-done(((bf16[8,4096]{1,0:T(8,128)(2,1)}), bf16[8,4096]{1,0:T(8,128)(2,1)}) %all-reduce.6.cloned.1.call-update) | async-done | bytes 65552 | tf_op jit(solution)/shard_map/while/body/eval_jaxpr/psum | solution.py:153
  698.7 36.8 %reduce-scatter.2.cloned.1.call-done = f32[8,640]{1,0:T(8,128)} async-done(((f32[8,5120]{1,0:T(8,128)}), f32[8,640]{1,0:T(8,128)}) %reduce-scatter.2.cloned.1.call-update) | async-done | bytes 20496 | tf_op jit(solution)/shard_map/while/body/eval_jaxpr/reduce_scatter | solution.py:123
  755.5 74.6 %all-reduce.6.cloned.1.call-done = bf16[8,4096]{1,0:T(8,128)(2,1)} async-done(((bf16[8,4096]{1,0:T(8,128)(2,1)}), bf16[8,4096]{1,0:T(8,128)(2,1)}) %all-reduce.6.cloned.1.call-update) | async-done | bytes 65552 | tf_op jit(solution)/shard_map/while/body/eval_jaxpr/psum | solution.py:153
  864.5 36.8 %reduce-scatter.2.cloned.1.call-done = f32[8,640]{1,0:T(8,128)} async-done(((f32[8,5120]{1,0:T(8,128)}), f32[8,640]{1,0:T(8,128)}) %reduce-scatter.2.cloned.1.call-update) | async-done | bytes 20496 | tf_op jit(solution)/shard_map/while/body/eval_jaxpr/reduce_scatter | solution.py:123
  921.3 72.2 %all-reduce.6.cloned.1.call-done = bf16[8,4096]{1,0:T(8,128)(2,1)} async-done(((bf16[8,4096]{1,0:T(8,128)(2,1)}), bf16[8,4096]{1,0:T(8,128)(2,1)}) %all-reduce.6.cloned.1.call-update) | async-done | bytes 65552 | tf_op jit(solution)/shard_map/while/body/eval_jaxpr/psum | solution.py:153
  1028.0 36.8 %reduce-scatter.2.cloned.1.call-done = f32[8,640]{1,0:T(8,128)} async-done(((f32[8,5120]{1,0:T(8,128)}), f32[8,640]{1,0:T(8,128)}) %reduce-scatter.2.cloned.1.call-update) | async-done | bytes 20496 | tf_op jit(solution)/shard_map/while/body/eval_jaxpr/reduce_scatter | solution.py:123
  1084.8 68.2 %all-reduce.6.cloned.1.call-done = bf16[8,4096]{1,0:T(8,128)(2,1)} async-done(((bf16[8,4096]{1,0:T(8,128)(2,1)}), bf16[8,4096]{1,0:T(8,128)(2,1)}) %all-reduce.6.cloned.1.call-update) | async-done | bytes 65552 | tf_op jit(solution)/shard_map/while/body/eval_jaxpr/psum | solution.py:153
  1159.0 32.6 %all-reduce.4.cloned.1.call-done = bf16[32,1024]{1,0:T(8,128)(2,1)} async-done(((bf16[32,1024]{1,0:T(8,128)(2,1)}), bf16[32,1024]{1,0:T(8,128)(2,1)}) %all-reduce.4.cloned.1.call-update) | async-done | bytes 65552 | tf_op jit(solution)/shard_map/psum | solution.py:24
  1192.6 21.4 %psum.57 = f32[32]{0:T(128)S(1)} all-reduce(f32[32]{0:T(128)S(1)} %fusion.50), channel_id=1, replica_groups=mesh['pipe'=4,'mp'=8] {'mp'}, use_global_device_ids=true, to_apply=%region_15.16 | all-reduce | flops 32 | bytes 256 | tf_op jit(solution)/shard_map/psum | solution.py:176
  1214.9 31.4 %all_gather.3 = bf16[32,8192]{1,0:T(8,128)(2,1)S(1)} all-gather(bf16[32,1024]{1,0:T(8,128)(2,1)S(1)} %fusion.49), channel_id=1, replica_groups=mesh['pipe'=4,'mp'=8] {'mp'}, dimensions={1}, use_global_device_ids=true | all-gather | bytes 589824 | tf_op jit(solution)/shard_map/all_gather | solution.py:181
  1250.2 36.8 %pmax.7 = f32[32]{0:T(128)S(1)} all-reduce(f32[32]{0:T(128)S(1)} %get-tuple-element.743), channel_id=1, replica_groups=mesh['pipe'=4,'mp'=8] {'pipe','mp'}, use_global_device_ids=true, to_apply=%region_17.18 | all-reduce | flops 32 | bytes 256 | tf_op jit(solution)/shard_map/pmax | solution.py:193
  1287.3 41.2 %all-reduce = (f32[32]{0:T(128)S(1)}, f32[32]{0:T(128)S(1)}) all-reduce(f32[32]{0:T(128)S(1)} %get-tuple-element.666, f32[32]{0:T(128)S(1)} %get-tuple-element.665), channel_id=1, replica_groups=mesh['pipe'=4,'mp'=8] {'pipe','mp'}, use_global_device_ids=true, to_apply=%region_19.20 | all-reduce | flops 64 | bytes 512 | tf_op jit(solution)/shard_map/psum | solution.py:195
  (450 shorter events, 370.7 us)
Async XLA Ops:
  13.6 69.5 %reduce-scatter.2.cloned.1.call-start = ((), (), s32[]{:S(2)}) async-start(), calls=%async_computation.3 | async-start | bytes 184320 | tf_op jit(solution)/shard_map/while/body/eval_jaxpr/reduce_scatter | solution.py:123
  13.7 4.1 collective-permute-start
  84.7 10.6 all-to-all-start
  88.3 85.6 %all-reduce.6.cloned.1.call-start = ((), (), s32[]{:S(2)}) async-start(), calls=%async_computation.4 | async-start | bytes 131072 | tf_op jit(solution)/shard_map/while/body/eval_jaxpr/psum | solution.py:153
  178.5 66.7 %reduce-scatter.2.cloned.1.call-start = ((), (), s32[]{:S(2)}) async-start(), calls=%async_computation.3 | async-start | bytes 184320 | tf_op jit(solution)/shard_map/while/body/eval_jaxpr/reduce_scatter | solution.py:123
  246.8 10.6 all-to-all-start
  250.4 85.5 %all-reduce.6.cloned.1.call-start = ((), (), s32[]{:S(2)}) async-start(), calls=%async_computation.4 | async-start | bytes 131072 | tf_op jit(solution)/shard_map/while/body/eval_jaxpr/psum | solution.py:153
  340.5 66.7 %reduce-scatter.2.cloned.1.call-start = ((), (), s32[]{:S(2)}) async-start(), calls=%async_computation.3 | async-start | bytes 184320 | tf_op jit(solution)/shard_map/while/body/eval_jaxpr/reduce_scatter | solution.py:123
  408.8 10.6 all-to-all-start
  412.4 88.4 %all-reduce.6.cloned.1.call-start = ((), (), s32[]{:S(2)}) async-start(), calls=%async_computation.4 | async-start | bytes 131072 | tf_op jit(solution)/shard_map/while/body/eval_jaxpr/psum | solution.py:153
  505.5 66.7 %reduce-scatter.2.cloned.1.call-start = ((), (), s32[]{:S(2)}) async-start(), calls=%async_computation.3 | async-start | bytes 184320 | tf_op jit(solution)/shard_map/while/body/eval_jaxpr/reduce_scatter | solution.py:123
  505.5 3.0 collective-permute-start
  573.8 10.6 all-to-all-start
  577.4 86.8 %all-reduce.6.cloned.1.call-start = ((), (), s32[]{:S(2)}) async-start(), calls=%async_computation.4 | async-start | bytes 131072 | tf_op jit(solution)/shard_map/while/body/eval_jaxpr/psum | solution.py:153
  668.8 66.7 %reduce-scatter.2.cloned.1.call-start = ((), (), s32[]{:S(2)}) async-start(), calls=%async_computation.3 | async-start | bytes 184320 | tf_op jit(solution)/shard_map/while/body/eval_jaxpr/reduce_scatter | solution.py:123
  737.1 10.6 all-to-all-start
  740.7 89.3 %all-reduce.6.cloned.1.call-start = ((), (), s32[]{:S(2)}) async-start(), calls=%async_computation.4 | async-start | bytes 131072 | tf_op jit(solution)/shard_map/while/body/eval_jaxpr/psum | solution.py:153
  834.7 66.7 %reduce-scatter.2.cloned.1.call-start = ((), (), s32[]{:S(2)}) async-start(), calls=%async_computation.3 | async-start | bytes 184320 | tf_op jit(solution)/shard_map/while/body/eval_jaxpr/reduce_scatter | solution.py:123
  902.9 10.6 all-to-all-start
  906.6 86.9 %all-reduce.6.cloned.1.call-start = ((), (), s32[]{:S(2)}) async-start(), calls=%async_computation.4 | async-start | bytes 131072 | tf_op jit(solution)/shard_map/while/body/eval_jaxpr/psum | solution.py:153
  998.1 66.7 %reduce-scatter.2.cloned.1.call-start = ((), (), s32[]{:S(2)}) async-start(), calls=%async_computation.3 | async-start | bytes 184320 | tf_op jit(solution)/shard_map/while/body/eval_jaxpr/reduce_scatter | solution.py:123
  1066.4 10.6 all-to-all-start
  1070.0 83.0 %all-reduce.6.cloned.1.call-start = ((), (), s32[]{:S(2)}) async-start(), calls=%async_computation.4 | async-start | bytes 131072 | tf_op jit(solution)/shard_map/while/body/eval_jaxpr/psum | solution.py:153
  1157.6 34.1 %all-reduce.4.cloned.1.call-start = ((), (), s32[]{:S(2)}) async-start(), calls=%async_computation.2 | async-start | bytes 131072 | tf_op jit(solution)/shard_map/psum | solution.py:24
  (7 other events, 2310.1 us)
Sparse Core Ops, SparseCore 0:
  24.2 58.8 reduce-scatter.1
  108.6 65.2 all-reduce.5
  188.0 57.1 reduce-scatter.1
  270.8 65.1 all-reduce.5
  350.0 57.1 reduce-scatter.1
  427.3 73.5 all-reduce.5
  515.0 57.1 reduce-scatter.1
  592.2 71.9 all-reduce.5
  678.3 57.1 reduce-scatter.1
  755.6 74.4 all-reduce.5
  844.1 57.1 reduce-scatter.1
  921.4 72.0 all-reduce.5
  1007.6 57.1 reduce-scatter.1
  1084.9 68.0 all-reduce.5
Sparse Core Ops, SparseCore 1:
  1160.4 31.2 all-reduce.3
where the time goes:
time: 1340 us
  waiting for transfers between devices  830 us (62%)
  blocking collectives  276 us (21%)
  matrix products  102 us (8%)
  local copies, waits for them, and re-layouts  43.2 us (3%)
  starting transfers between devices  35.9 us (3%)
  loops' own time  22.4 us (2%)
  between operations  15.3 us (1%)
    psum x7, waiting for transfers between devices, apply_layer(): gathered = lax.psum(spread.astype(jnp.bfloat16), 'mp')  491 us
    reduce_scatter x7, waiting for transfers between devices, apply_layer(): lax.psum_scatter(partial_cols, 'mp', scatter_dimension=1, tiled=True)  257 us
    psum x7, blocking collectives, apply_layer(): squares_all = lax.psum(squares, 'mp')  145 us
    all_to_all x7, waiting for transfers between devices, apply_layer(): lax.all_to_all(routed_rows, 'mp', split_axis=0, concat_axis=1, tiled=True)  48.7 us
    dot_general x7, matrix products, apply_layer(): jnp.dot(scaled, weight_in, preferred_element_type=jnp.float32)  42.7 us
    psum x1, blocking collectives, local(): row_total, picked = lax.psum((local_total, picked_local), ('pipe', 'mp'))  41.2 us
    pmax x1, blocking collectives, local(): row_top = lax.pmax(local_top, ('pipe', 'mp'))  36.8 us
    psum x1, waiting for transfers between devices, from_root(): return lax.psum(jnp.where(mine, value, jnp.zeros_like(value)), axis)  32.6 us
  transfers between devices with their start and end apart: 29, of which 22 were waited for; matrix products, arithmetic and copies ran while one was open for 1% of the time, Pallas kernels for 0%

commit v1 on v0

--- a/solution.py
+++ b/solution.py
@@ -150,7 +150,8 @@
             jnp.bfloat16
         )
         spread = jnp.dot(placing.T, attended, preferred_element_type=jnp.float32)
-        gathered = lax.psum(spread.astype(jnp.bfloat16), "mp")
+        mine_x = spread.astype(jnp.bfloat16)
+        gathered = jnp.sum(jax.lax.all_gather(mine_x, "mp"), 0)
         update = jnp.dot(gathered, weight_out, preferred_element_type=jnp.float32)
         return (current + update).astype(jnp.bfloat16)
 

time: 1340 us -> 1060 us (0.79)
  waiting for transfers between devices: 830 us -> 341 us
  blocking collectives: 276 us -> 491 us
    psum x7 -> x0, waiting for transfers between devices: 491 us -> none  [apply_layer(): gathered = lax.psum(spread.astype(jnp.bfloat16), 'mp')]
    all_gather x0 -> x7, blocking collectives: none -> 225 us  [apply_layer(): gathered = jnp.sum(jax.lax.all_gather(mine_x, 'mp'), 0)]
  transfers between devices with their start and end apart: 29 -> 22, of which waited for: 22 -> 15; matrix products, arithmetic and copies ran while one was open for 1% -> 1% of each run, Pallas kernels for 0% -> 0%
where the time goes in v1:
time: 1060 us
  blocking collectives  491 us (46%)
  waiting for transfers between devices  341 us (32%)
  matrix products  97.3 us (9%)
  local copies, waits for them, and re-layouts  43.2 us (4%)
  starting transfers between devices  35.7 us (3%)
  loops' own time  22.3 us (2%)
  between operations  15.6 us (1%)
  other arithmetic  12.8 us (1%)
    reduce_scatter x7, waiting for transfers between devices, apply_layer(): lax.psum_scatter(partial_cols, 'mp', scatter_dimension=1, tiled=True)  262 us
    all_gather x7, blocking collectives, apply_layer(): gathered = jnp.sum(jax.lax.all_gather(mine_x, 'mp'), 0)  225 us
    psum x7, blocking collectives, apply_layer(): squares_all = lax.psum(squares, 'mp')  135 us
    all_to_all x7, waiting for transfers between devices, apply_layer(): lax.all_to_all(routed_rows, 'mp', split_axis=0, concat_axis=1, tiled=True)  49.1 us
    dot_general x7, matrix products, apply_layer(): jnp.dot(scaled, weight_in, preferred_element_type=jnp.float32)  42.7 us
    psum x1, blocking collectives, local(): row_total, picked = lax.psum((local_total, picked_local), ('pipe', 'mp'))  41.2 us
    pmax x1, blocking collectives, local(): row_top = lax.pmax(local_top, ('pipe', 'mp'))  36.9 us
    dot_general x7, matrix products, apply_layer(): update = jnp.dot(gathered, weight_out, preferred_element_type=jnp.float32)  32.1 us
  transfers between devices with their start and end apart: 22, of which 15 were waited for; matrix products, arithmetic and copies ran while one was open for 1% of the time, Pallas kernels for 0%

profile of v1, /device:TPU:0, one launch (start us, length us, event | category | flops | bytes accessed | tf_op | source)
XLA Modules:
  0.0 1059.0 jit_solution(7733927840864328642)
XLA Ops:
  13.6 868.2 %while.53 = (s32[]{:T(128)}, bf16[8,1024]{1,0:T(8,128)(2,1)S(1)}, bf16[32,1024]{1,0:T(8,128)(2,1)S(1)}, pred[]{:T(512)}, s32[]{:T(128)}, /*index=5*/s32[4,8]{1,0...) while((s32[]{:T(128)}, bf16[8,1024]{1,0:T(8,128)(2,1)S(1)}, ...), condition=%wide.region_12.13_spmd.clone.clone, body=%wide.region_1.12_spmd.clone.clone.sunk | while | flops 158046032 | bytes 22922740 | solution.py:174
  24.2 22.5 %psum.49 = f32[8]{0:T(128)S(1)} all-reduce(f32[8]{0:T(128)S(1)} %get-tuple-element.930), channel_id=1, replica_groups=mesh['pipe'=4,'mp'=8] {'mp'}, use_global_device_ids=true, to_apply=%region_4.4 | all-reduce | flops 8 | bytes 64 | tf_op jit(solution)/shard_map/while/body/eval_jaxpr/psum | solution.py:122
  46.7 36.4 %reduce-scatter.2.cloned.1.call-done = f32[8,640]{1,0:T(8,128)} async-done(((f32[8,5120]{1,0:T(8,128)}), f32[8,640]{1,0:T(8,128)}) %reduce-scatter.2.cloned.1.call-update) | async-done | bytes 20496 | tf_op jit(solution)/shard_map/while/body/eval_jaxpr/reduce_scatter | solution.py:123
  107.9 31.3 %all-gather.3 = bf16[64,4096]{1,0:T(8,128)(2,1)S(1)} all-gather(bf16[8,4096]{1,0:T(8,128)(2,1)S(1)} %convolution_convert_fusion.2), channel_id=2, replica_groups=mesh['pipe'=4,'mp'=8] {'mp'}, dimensions={0}, use_global_device_ids=true | all-gather | bytes 589824 | tf_op jit(solution)/shard_map/while/body/eval_jaxpr/all_gather | solution.py:154
  170.6 34.2 %reduce-scatter.2.cloned.1.call-done = f32[8,640]{1,0:T(8,128)} async-done(((f32[8,5120]{1,0:T(8,128)}), f32[8,640]{1,0:T(8,128)}) %reduce-scatter.2.cloned.1.call-update) | async-done | bytes 20496 | tf_op jit(solution)/shard_map/while/body/eval_jaxpr/reduce_scatter | solution.py:123
  229.6 31.3 %all-gather.3 = bf16[64,4096]{1,0:T(8,128)(2,1)S(1)} all-gather(bf16[8,4096]{1,0:T(8,128)(2,1)S(1)} %convolution_convert_fusion.2), channel_id=2, replica_groups=mesh['pipe'=4,'mp'=8] {'mp'}, dimensions={0}, use_global_device_ids=true | all-gather | bytes 589824 | tf_op jit(solution)/shard_map/while/body/eval_jaxpr/all_gather | solution.py:154
  292.5 34.1 %reduce-scatter.2.cloned.1.call-done = f32[8,640]{1,0:T(8,128)} async-done(((f32[8,5120]{1,0:T(8,128)}), f32[8,640]{1,0:T(8,128)}) %reduce-scatter.2.cloned.1.call-update) | async-done | bytes 20496 | tf_op jit(solution)/shard_map/while/body/eval_jaxpr/reduce_scatter | solution.py:123
  345.9 35.2 %all-gather.3 = bf16[64,4096]{1,0:T(8,128)(2,1)S(1)} all-gather(bf16[8,4096]{1,0:T(8,128)(2,1)S(1)} %convolution_convert_fusion.2), channel_id=2, replica_groups=mesh['pipe'=4,'mp'=8] {'mp'}, dimensions={0}, use_global_device_ids=true | all-gather | bytes 589824 | tf_op jit(solution)/shard_map/while/body/eval_jaxpr/all_gather | solution.py:154
  395.2 21.8 %psum.49 = f32[8]{0:T(128)S(1)} all-reduce(f32[8]{0:T(128)S(1)} %get-tuple-element.930), channel_id=1, replica_groups=mesh['pipe'=4,'mp'=8] {'mp'}, use_global_device_ids=true, to_apply=%region_4.4 | all-reduce | flops 8 | bytes 64 | tf_op jit(solution)/shard_map/while/body/eval_jaxpr/psum | solution.py:122
  417.0 34.2 %reduce-scatter.2.cloned.1.call-done = f32[8,640]{1,0:T(8,128)} async-done(((f32[8,5120]{1,0:T(8,128)}), f32[8,640]{1,0:T(8,128)}) %reduce-scatter.2.cloned.1.call-update) | async-done | bytes 20496 | tf_op jit(solution)/shard_map/while/body/eval_jaxpr/reduce_scatter | solution.py:123
  470.5 32.3 %all-gather.3 = bf16[64,4096]{1,0:T(8,128)(2,1)S(1)} all-gather(bf16[8,4096]{1,0:T(8,128)(2,1)S(1)} %convolution_convert_fusion.2), channel_id=2, replica_groups=mesh['pipe'=4,'mp'=8] {'mp'}, dimensions={0}, use_global_device_ids=true | all-gather | bytes 589824 | tf_op jit(solution)/shard_map/while/body/eval_jaxpr/all_gather | solution.py:154
  517.0 20.3 %psum.49 = f32[8]{0:T(128)S(1)} all-reduce(f32[8]{0:T(128)S(1)} %get-tuple-element.930), channel_id=1, replica_groups=mesh['pipe'=4,'mp'=8] {'mp'}, use_global_device_ids=true, to_apply=%region_4.4 | all-reduce | flops 8 | bytes 64 | tf_op jit(solution)/shard_map/while/body/eval_jaxpr/psum | solution.py:122
  537.3 38.9 %reduce-scatter.2.cloned.1.call-done = f32[8,640]{1,0:T(8,128)} async-done(((f32[8,5120]{1,0:T(8,128)}), f32[8,640]{1,0:T(8,128)}) %reduce-scatter.2.cloned.1.call-update) | async-done | bytes 20496 | tf_op jit(solution)/shard_map/while/body/eval_jaxpr/reduce_scatter | solution.py:123
  595.5 31.8 %all-gather.3 = bf16[64,4096]{1,0:T(8,128)(2,1)S(1)} all-gather(bf16[8,4096]{1,0:T(8,128)(2,1)S(1)} %convolution_convert_fusion.2), channel_id=2, replica_groups=mesh['pipe'=4,'mp'=8] {'mp'}, dimensions={0}, use_global_device_ids=true | all-gather | bytes 589824 | tf_op jit(solution)/shard_map/while/body/eval_jaxpr/all_gather | solution.py:154
  659.2 44.1 %reduce-scatter.2.cloned.1.call-done = f32[8,640]{1,0:T(8,128)} async-done(((f32[8,5120]{1,0:T(8,128)}), f32[8,640]{1,0:T(8,128)}) %reduce-scatter.2.cloned.1.call-update) | async-done | bytes 20496 | tf_op jit(solution)/shard_map/while/body/eval_jaxpr/reduce_scatter | solution.py:123
  722.6 31.5 %all-gather.3 = bf16[64,4096]{1,0:T(8,128)(2,1)S(1)} all-gather(bf16[8,4096]{1,0:T(8,128)(2,1)S(1)} %convolution_convert_fusion.2), channel_id=2, replica_groups=mesh['pipe'=4,'mp'=8] {'mp'}, dimensions={0}, use_global_device_ids=true | all-gather | bytes 589824 | tf_op jit(solution)/shard_map/while/body/eval_jaxpr/all_gather | solution.py:154
  768.3 18.0 %psum.49 = f32[8]{0:T(128)S(1)} all-reduce(f32[8]{0:T(128)S(1)} %get-tuple-element.930), channel_id=1, replica_groups=mesh['pipe'=4,'mp'=8] {'mp'}, use_global_device_ids=true, to_apply=%region_4.4 | all-reduce | flops 8 | bytes 64 | tf_op jit(solution)/shard_map/while/body/eval_jaxpr/psum | solution.py:122
  786.3 40.0 %reduce-scatter.2.cloned.1.call-done = f32[8,640]{1,0:T(8,128)} async-done(((f32[8,5120]{1,0:T(8,128)}), f32[8,640]{1,0:T(8,128)}) %reduce-scatter.2.cloned.1.call-update) | async-done | bytes 20496 | tf_op jit(solution)/shard_map/while/body/eval_jaxpr/reduce_scatter | solution.py:123
  845.6 31.5 %all-gather.3 = bf16[64,4096]{1,0:T(8,128)(2,1)S(1)} all-gather(bf16[8,4096]{1,0:T(8,128)(2,1)S(1)} %convolution_convert_fusion.2), channel_id=2, replica_groups=mesh['pipe'=4,'mp'=8] {'mp'}, dimensions={0}, use_global_device_ids=true | all-gather | bytes 589824 | tf_op jit(solution)/shard_map/while/body/eval_jaxpr/all_gather | solution.py:154
  883.2 30.3 %all-reduce.3.cloned.1.call-done = bf16[32,1024]{1,0:T(8,128)(2,1)} async-done(((bf16[32,1024]{1,0:T(8,128)(2,1)}), bf16[32,1024]{1,0:T(8,128)(2,1)}) %all-reduce.3.cloned.1.call-update) | async-done | bytes 65552 | tf_op jit(solution)/shard_map/psum | solution.py:24
  914.5 21.4 %psum.43 = f32[32]{0:T(128)S(1)} all-reduce(f32[32]{0:T(128)S(1)} %fusion.50), channel_id=1, replica_groups=mesh['pipe'=4,'mp'=8] {'mp'}, use_global_device_ids=true, to_apply=%region_15.16 | all-reduce | flops 32 | bytes 256 | tf_op jit(solution)/shard_map/psum | solution.py:177
  936.8 31.4 %all_gather.23 = bf16[32,8192]{1,0:T(8,128)(2,1)S(1)} all-gather(bf16[32,1024]{1,0:T(8,128)(2,1)S(1)} %fusion.49), channel_id=1, replica_groups=mesh['pipe'=4,'mp'=8] {'mp'}, dimensions={1}, use_global_device_ids=true | all-gather | bytes 589824 | tf_op jit(solution)/shard_map/all_gather | solution.py:182
  972.1 36.9 %pmax.7 = f32[32]{0:T(128)S(1)} all-reduce(f32[32]{0:T(128)S(1)} %get-tuple-element.744), channel_id=1, replica_groups=mesh['pipe'=4,'mp'=8] {'pipe','mp'}, use_global_device_ids=true, to_apply=%region_17.18 | all-reduce | flops 32 | bytes 256 | tf_op jit(solution)/shard_map/pmax | solution.py:194
  1009.1 41.2 %all-reduce = (f32[32]{0:T(128)S(1)}, f32[32]{0:T(128)S(1)}) all-reduce(f32[32]{0:T(128)S(1)} %get-tuple-element.667, f32[32]{0:T(128)S(1)} %get-tuple-element.666), channel_id=1, replica_groups=mesh['pipe'=4,'mp'=8] {'pipe','mp'}, use_global_device_ids=true, to_apply=%region_19.20 | all-reduce | flops 64 | bytes 512 | tf_op jit(solution)/shard_map/psum | solution.py:196
  (443 shorter events, 357.9 us)
Async XLA Ops:
  8.0 874.5 %copy-start = (s32[32]{0:T(128)S(1)}, s32[32]{0:T(128)}, u32[]{:S(2)}) copy-start(s32[32]{0:T(128)} %param.20) | copy-start | bytes 388
  13.6 868.9 %copy-start.1 = (bf16[1024]{0:T(1024)(128)(2,1)S(1)}, bf16[1024]{0:T(1024)(128)(2,1)}, u32[]{:S(2)}) copy-start(bf16[1024]{0:T(1024)(128)(2,1)} %param.26) | copy-start | bytes 6148
  13.6 69.5 %reduce-scatter.2.cloned.1.call-start = ((), (), s32[]{:S(2)}) async-start(), calls=%async_computation.3 | async-start | bytes 184320 | tf_op jit(solution)/shard_map/while/body/eval_jaxpr/reduce_scatter | solution.py:123
  13.7 4.1 collective-permute-start
  84.7 10.6 %all-to-all-start = ((f32[8,4,640]{2,1,0:T(4,128)}), f32[8,4,640]{2,1,0:T(4,128)S(1)}, u32[]{:S(2)}, u32[]{:S(2)}) async-start(f32[8,4,640]{2,1,0:T(4,128)} %all_to_all.47), calls=%async_computation.1 | async-start | bytes 163840 | tf_op jit(solution)/shard_map/while/body/eval_jaxpr/all_to_all | solution.py:133
  143.8 61.0 %reduce-scatter.2.cloned.1.call-start = ((), (), s32[]{:S(2)}) async-start(), calls=%async_computation.3 | async-start | bytes 184320 | tf_op jit(solution)/shard_map/while/body/eval_jaxpr/reduce_scatter | solution.py:123
  143.8 3.0 collective-permute-start
  206.4 10.6 %all-to-all-start = ((f32[8,4,640]{2,1,0:T(4,128)}), f32[8,4,640]{2,1,0:T(4,128)S(1)}, u32[]{:S(2)}, u32[]{:S(2)}) async-start(f32[8,4,640]{2,1,0:T(4,128)} %all_to_all.47), calls=%async_computation.1 | async-start | bytes 163840 | tf_op jit(solution)/shard_map/while/body/eval_jaxpr/all_to_all | solution.py:133
  265.6 61.0 %reduce-scatter.2.cloned.1.call-start = ((), (), s32[]{:S(2)}) async-start(), calls=%async_computation.3 | async-start | bytes 184320 | tf_op jit(solution)/shard_map/while/body/eval_jaxpr/reduce_scatter | solution.py:123
  265.6 3.0 collective-permute-start
  328.2 10.6 %all-to-all-start = ((f32[8,4,640]{2,1,0:T(4,128)}), f32[8,4,640]{2,1,0:T(4,128)S(1)}, u32[]{:S(2)}, u32[]{:S(2)}) async-start(f32[8,4,640]{2,1,0:T(4,128)} %all_to_all.47), calls=%async_computation.1 | async-start | bytes 163840 | tf_op jit(solution)/shard_map/while/body/eval_jaxpr/all_to_all | solution.py:133
  385.7 65.5 %reduce-scatter.2.cloned.1.call-start = ((), (), s32[]{:S(2)}) async-start(), calls=%async_computation.3 | async-start | bytes 184320 | tf_op jit(solution)/shard_map/while/body/eval_jaxpr/reduce_scatter | solution.py:123
  385.7 3.0 collective-permute-start
  452.8 10.7 %all-to-all-start = ((f32[8,4,640]{2,1,0:T(4,128)}), f32[8,4,640]{2,1,0:T(4,128)S(1)}, u32[]{:S(2)}, u32[]{:S(2)}) async-start(f32[8,4,640]{2,1,0:T(4,128)} %all_to_all.47), calls=%async_computation.1 | async-start | bytes 163840 | tf_op jit(solution)/shard_map/while/body/eval_jaxpr/all_to_all | solution.py:133
  507.5 68.7 %reduce-scatter.2.cloned.1.call-start = ((), (), s32[]{:S(2)}) async-start(), calls=%async_computation.3 | async-start | bytes 184320 | tf_op jit(solution)/shard_map/while/body/eval_jaxpr/reduce_scatter | solution.py:123
  507.5 3.0 collective-permute-start
  577.8 10.6 %all-to-all-start = ((f32[8,4,640]{2,1,0:T(4,128)}), f32[8,4,640]{2,1,0:T(4,128)S(1)}, u32[]{:S(2)}, u32[]{:S(2)}) async-start(f32[8,4,640]{2,1,0:T(4,128)} %all_to_all.47), calls=%async_computation.1 | async-start | bytes 163840 | tf_op jit(solution)/shard_map/while/body/eval_jaxpr/all_to_all | solution.py:133
  632.0 71.3 %reduce-scatter.2.cloned.1.call-start = ((), (), s32[]{:S(2)}) async-start(), calls=%async_computation.3 | async-start | bytes 184320 | tf_op jit(solution)/shard_map/while/body/eval_jaxpr/reduce_scatter | solution.py:123
  632.0 3.0 collective-permute-start
  704.9 10.7 %all-to-all-start = ((f32[8,4,640]{2,1,0:T(4,128)}), f32[8,4,640]{2,1,0:T(4,128)S(1)}, u32[]{:S(2)}, u32[]{:S(2)}) async-start(f32[8,4,640]{2,1,0:T(4,128)} %all_to_all.47), calls=%async_computation.1 | async-start | bytes 163840 | tf_op jit(solution)/shard_map/while/body/eval_jaxpr/all_to_all | solution.py:133
  758.8 67.5 %reduce-scatter.2.cloned.1.call-start = ((), (), s32[]{:S(2)}) async-start(), calls=%async_computation.3 | async-start | bytes 184320 | tf_op jit(solution)/shard_map/while/body/eval_jaxpr/reduce_scatter | solution.py:123
  758.8 3.0 collective-permute-start
  827.9 10.7 %all-to-all-start = ((f32[8,4,640]{2,1,0:T(4,128)}), f32[8,4,640]{2,1,0:T(4,128)S(1)}, u32[]{:S(2)}, u32[]{:S(2)}) async-start(f32[8,4,640]{2,1,0:T(4,128)} %all_to_all.47), calls=%async_computation.1 | async-start | bytes 163840 | tf_op jit(solution)/shard_map/while/body/eval_jaxpr/all_to_all | solution.py:133
  881.8 31.8 %all-reduce.3.cloned.1.call-start = ((), (), s32[]{:S(2)}) async-start(), calls=%async_computation.2 | async-start | bytes 131072 | tf_op jit(solution)/shard_map/psum | solution.py:24
Sparse Core Ops, SparseCore 0:
  24.2 58.8 reduce-scatter.1
  153.3 51.4 reduce-scatter.1
  275.0 51.4 reduce-scatter.1
  395.2 55.9 reduce-scatter.1
  517.0 59.1 reduce-scatter.1
  641.5 61.7 reduce-scatter.1
  768.3 57.9 reduce-scatter.1
Sparse Core Ops, SparseCore 1:
  884.6 28.9 all-reduce.2
